TPU v7x, 32 devices: a whole 2x2x4 slice. The times are simulated.
32 devices in a mesh: row: 8 (over z, y), col: 4 (over x, core).
Axes of the slice: x: 2, y: 2, z: 4, core: 2. Of those that a mesh axis runs over, the one named last changes fastest.
Arguments:
- features: float32 [32, 3072], P(None, ('row', 'col')), may hold values from -6 to 6
- block: float32 [16, 3072], P(None, ('row', 'col')), may hold values from -6 to 6
Outputs:
- applied: float32 [16, 3072], P(None, ('row', 'col'))
All inputs are finite; a program needn't handle non-finite values.
Results may differ from a plain program's by a relative error of at most 0.006.
Values may be sent and summed in bfloat16 or wider, within the bound.
A program may use at most 64 MiB of HBM per device.

v0:
```python
import math
import jax
import jax.numpy as jnp
from jax import lax
from jax.sharding import PartitionSpec as P


def kernel_rows(row_feat, row_sq, col_feat, col_sq, scale, start, count):
    part = lax.dynamic_slice_in_dim(row_feat, start, count, 1)
    sq_part = lax.dynamic_slice_in_dim(row_sq, start, count, 0)
    inner = jnp.einsum("fi,fj->ij", part, col_feat, precision=lax.Precision.HIGHEST)
    dist = sq_part[:, None] + col_sq[None, :] - 2.0 * inner
    return jnp.exp(-dist / scale).astype(jnp.bfloat16)


def combine(partial_value, owned):
    whole = lax.psum(partial_value, "col")
    return lax.dynamic_slice_in_dim(whole, lax.axis_index("col") * owned, owned, 1)


def full_plan(features, block, row_feat, scale):
    owned = features.shape[1]
    col_feat = lax.all_gather(features, "row", axis=1, tiled=True)
    row_sq = jnp.sum(row_feat * row_feat, axis=0)
    col_sq = jnp.sum(col_feat * col_feat, axis=0)
    rows = row_feat.shape[1]
    step = math.gcd(512, rows)
    count_blocks = rows // step
    starts = jnp.arange(count_blocks, dtype=jnp.int32) * step
    indexes = jnp.arange(count_blocks, dtype=jnp.int32)

    def fetch(index):
        return kernel_rows(row_feat, row_sq, col_feat, col_sq, scale, starts[index], step)

    def first_pass(index):
        tile = fetch(index)
        return (jnp.sum(tile, axis=1, dtype=jnp.float32), jnp.sum(tile, axis=0, dtype=jnp.float32))

    row_parts, col_parts = lax.map(first_pass, indexes)
    q_own = combine(row_parts.reshape(1, rows), owned)
    inv_own = 1.0 / q_own
    col_total = lax.psum(jnp.sum(col_parts, axis=0)[None, :], "row")
    inv_col = 1.0 / col_total

    def second_pass(index):
        return jnp.sum(fetch(index).astype(jnp.float32) * inv_col, axis=1)

    second = combine(lax.map(second_pass, indexes).reshape(1, rows), owned)
    dens = second * inv_own
    factor = inv_own * lax.rsqrt(dens)
    weighted = (block * factor).astype(jnp.bfloat16)
    weighted_col = lax.all_gather(weighted, "row", axis=1, tiled=True)

    def third_pass(index):
        return jnp.einsum(
            "kj,ij->ki", weighted_col, fetch(index), preferred_element_type=jnp.float32
        )

    products = lax.map(third_pass, indexes)
    partial_value = jnp.moveaxis(products, 0, 1).reshape(block.shape[0], rows)
    return combine(partial_value, owned) * factor


def per_device(features, block):
    n_row = lax.axis_size("row")
    n_col = lax.axis_size("col")
    width, owned = features.shape
    frames = owned * n_row * n_col
    scale = 4.0 / (float(frames) ** (2.0 / width) - 1.0)
    row_feat = lax.all_gather(features, "col", axis=1, tiled=True)
    return full_plan(features, block, row_feat, scale)


def solution(mesh):
    placed = (P(None, ("row", "col")), P(None, ("row", "col")))
    return jax.shard_map(
        per_device, mesh=mesh, in_specs=placed, out_specs=P(None, ("row", "col")), check_vma=False
    )
```

profile of v0, /device:TPU:0, one launch (start us, length us, event | category | flops | bytes accessed | tf_op | source)
XLA Modules:
  0.0 166.0 jit_solution(17195008290931523014)
XLA Ops:
  0.0 32.5 %all-gather.1 = f32[8,96,32]{1,2,0:T(8,128)S(1)} all-gather(f32[1,96,32]{1,2,0:T(8,128)} %bitcast.84), channel_id=1, replica_groups=mesh['row'=8,'col'=4] {'row'}, dimensions={0}, use_global_device_ids=true | all-gather | bytes 110592 | tf_op jit(solution)/shard_map/all_gather | solution.py:23
  32.5 0.1 copy.13
  32.6 0.1 reshape.21
  32.8 0.7 copy-done
  33.4 5.2 %all-gather = f32[4,96,32]{1,2,0:T(8,128)S(1)} all-gather(f32[1,96,32]{1,2,0:T(8,128)S(1)} %bitcast.85), channel_id=1, replica_groups=mesh['row'=8,'col'=4] {'col'}, dimensions={0}, use_global_device_ids=true | all-gather | bytes 61440 | tf_op jit(solution)/shard_map/all_gather | solution.py:70
  38.7 0.1 reshape.19
  38.9 19.3 %while.32 = (s32[]{:T(128)}, f32[3,128]{1,0:T(4,128)S(1)}, f32[3,768]{1,0:T(4,128)S(1)}, s32[3]{0:T(128)S(1)}, s32[3]{0:T(128)S(1)}, /*index=5*/f32[384]{0:T(512...) while((s32[]{:T(128)}, f32[3,128]{1,0:T(4,128)S(1)}, ...), condition=%wide.region_5.6_spmd, body=%wide.region_2.5_spmd.sunk | while | flops 38632584 | bytes 137449 | solution.py:39
  38.9 0.7 dynamic_slice.87
  41.6 0.7 dynamic_slice.88
  44.4 0.1 dynamic_slice.89
  44.5 0.7 fusion.51
  45.3 0.7 dynamic_slice.87
  48.1 0.7 dynamic_slice.88
  50.9 0.7 fusion.51
  51.8 0.7 dynamic_slice.87
  54.5 0.7 dynamic_slice.88
  57.3 0.7 fusion.51
  58.2 21.4 %psum.29 = f32[1,768]{1,0:T(1,128)S(1)} all-reduce(f32[1,768]{1,0:T(1,128)S(1)} %broadcast_in_dim.32), channel_id=1, replica_groups=mesh['row'=8,'col'=4] {'row'}, use_global_device_ids=true, to_apply=%region_8.9 | all-reduce | flops 768 | bytes 6144 | tf_op jit(solution)/shard_map/psum | solution.py:42
  79.6 19.1 %while.33 = (s32[]{:T(128)}, f32[3,128]{1,0:T(4,128)S(1)}, s32[3]{0:T(128)S(1)}, s32[3]{0:T(128)S(1)}, f32[384]{0:T(512)S(1)}, /*index=5*/f32[768]{0:T(1024)S(1)...) while((s32[]{:T(128)}, f32[3,128]{1,0:T(4,128)S(1)}, ...), condition=%wide.region_11.12_spmd, body=%wide.region_9.11_spmd.sunk | while | flops 38633352 | bytes 132337 | solution.py:48
  79.6 0.7 dynamic_slice.91
  82.4 0.7 dynamic_slice.92
  85.2 0.7 fusion.54
  86.0 0.7 dynamic_slice.91
  88.7 0.7 dynamic_slice.92
  91.6 0.7 fusion.54
  92.3 0.7 dynamic_slice.91
  95.1 0.7 dynamic_slice.92
  97.9 0.7 fusion.54
  98.7 5.7 %all-reduce = (f32[1,384]{1,0:T(1,128)S(1)}, f32[1,384]{1,0:T(1,128)S(1)}) all-reduce(f32[1,384]{1,0:T(1,128)S(1)} %get-tuple-element.209, f32[1,384]{1,0:T(1,128)S(1)} %get-tuple-element.210), channel_id=1, replica_groups=mesh['row'=8,'col'=4] {'col'}, use_global_device_ids=true, to_apply=%region_12.13 | all-reduce | flops 768 | bytes 6144 | tf_op jit(solution)/shard_map/psum | solution.py:17
  104.5 0.6 copy-done.1
  105.1 30.6 %all-gather.2 = bf16[8,96,16]{1,2,0:T(8,128)(2,1)S(1)} all-gather(bf16[1,96,16]{1,2,0:T(8,128)(2,1)S(1)} %fusion.26), channel_id=1, replica_groups=mesh['row'=8,'col'=4] {'row'}, dimensions={0}, use_global_device_ids=true | all-gather | bytes 27648 | tf_op jit(solution)/shard_map/all_gather | solution.py:52
  135.7 0.1 reshape.23
  135.8 19.2 %while.34 = (s32[]{:T(128)}, f32[3,16,128]{2,1,0:T(8,128)S(1)}, s32[3]{0:T(128)S(1)}, s32[3]{0:T(128)S(1)}, f32[384]{0:T(512)S(1)}, /*index=5*/f32[768]{0:T(1024...) while((s32[]{:T(128)}, f32[3,16,128]{2,1,0:T(8,128)S(1)}, ...), condition=%wide.region_14.15_spmd, body=%wide.region_13.14_spmd.sunk | while | flops 41484296 | bytes 546533 | solution.py:59
  135.8 0.7 dynamic_slice.95
  138.6 0.7 dynamic_slice.96
  141.3 0.1 dynamic_slice.97
  141.4 0.6 fusion.59
  142.0 0.1 fusion.60
  142.2 0.7 dynamic_slice.95
  145.0 0.7 dynamic_slice.96
  147.8 0.6 fusion.59
  148.4 0.1 fusion.60
  148.6 0.7 dynamic_slice.95
  151.4 0.7 dynamic_slice.96
  154.2 0.6 fusion.59
  154.8 0.1 fusion.60
  155.0 10.3 %psum.31 = f32[16,384]{1,0:T(8,128)S(1)} all-reduce(f32[16,384]{1,0:T(8,128)S(1)} %copy_bitcast_fusion), channel_id=1, replica_groups=mesh['row'=8,'col'=4] {'col'}, use_global_device_ids=true, to_apply=%region_15.16 | all-reduce | flops 6144 | bytes 49152 | tf_op jit(solution)/shard_map/psum | solution.py:17
  165.3 0.7 dynamic-slice_multiply_fusion
  (43 shorter events, 1.3 us)
Async XLA Ops:
  32.7 0.7 copy-start
  104.4 0.7 copy-start.1
where the time goes:
time: 167 us; the launch traced here: 166 us
  blocking collectives  106 us (63%)
  loops' own time  37.5 us (22%)
  local copies, waits for them, and re-layouts  15 us (9%)
  matrix products  6.79 us (4%)
    all_gather x1, blocking collectives, full_plan(): col_feat = lax.all_gather(features, 'row', axis=1, tiled=True)  32.5 us
    all_gather x1, blocking collectives, full_plan(): weighted_col = lax.all_gather(weighted, 'row', axis=1, tiled=True)  30.6 us
    psum x1, blocking collectives, full_plan(): col_total = lax.psum(jnp.sum(col_parts, axis=0)[None, :], 'row')  21.4 us
    psum x2, blocking collectives, combine(): whole = lax.psum(partial_value, 'col')  16 us
    another operation x1, loops' own time, full_plan(): row_parts, col_parts = lax.map(first_pass, indexes)  12.5 us
    another operation x1, loops' own time, full_plan(): products = lax.map(third_pass, indexes)  12.5 us
    another operation x1, loops' own time, full_plan(): second = combine(lax.map(second_pass, indexes).reshape(1, rows), owned)  12.5 us
    dot_general x9, matrix products, kernel_rows(): jnp.einsum('fi,fj->ij', part, col_feat, precision=lax.Precision.HIGHEST)  6.41 us

commit v1 on v0

--- a/solution.py
+++ b/solution.py
@@ -39,7 +39,7 @@
     row_parts, col_parts = lax.map(first_pass, indexes)
     q_own = combine(row_parts.reshape(1, rows), owned)
     inv_own = 1.0 / q_own
-    col_total = lax.psum(jnp.sum(col_parts, axis=0)[None, :], "row")
+    col_total = jnp.sum(lax.all_gather(jnp.sum(col_parts, axis=0)[None, :], "row"), axis=0)
     inv_col = 1.0 / col_total
 
     def second_pass(index):

time: 167 us -> 176 us (1.054)
  blocking collectives: 106 us -> 115 us
    all_gather x0 -> x1, blocking collectives: none -> 30.5 us  [full_plan(): lax.all_gather(jnp.sum(col_parts, axis=0)[None, :], 'row')]
    psum x1 -> x0, blocking collectives: 21.4 us -> none  [full_plan(): col_total = lax.psum(jnp.sum(col_parts, axis=0)[None, :], 'row')]
where the time goes in v1:
time: 176 us; the launch traced here: 175 us
  blocking collectives  115 us (65%)
  loops' own time  37.5 us (21%)
  local copies, waits for them, and re-layouts  15 us (9%)
  matrix products  6.79 us (4%)
    all_gather x1, blocking collectives, full_plan(): col_feat = lax.all_gather(features, 'row', axis=1, tiled=True)  32.5 us
    all_gather x1, blocking collectives, full_plan(): weighted_col = lax.all_gather(weighted, 'row', axis=1, tiled=True)  30.6 us
    all_gather x1, blocking collectives, full_plan(): lax.all_gather(jnp.sum(col_parts, axis=0)[None, :], 'row')  30.5 us
    psum x2, blocking collectives, combine(): whole = lax.psum(partial_value, 'col')  16 us
    another operation x1, loops' own time, full_plan(): row_parts, col_parts = lax.map(first_pass, indexes)  12.5 us
    another operation x1, loops' own time, full_plan(): products = lax.map(third_pass, indexes)  12.5 us
    another operation x1, loops' own time, full_plan(): second = combine(lax.map(second_pass, indexes).reshape(1, rows), owned)  12.5 us
    dot_general x9, matrix products, kernel_rows(): jnp.einsum('fi,fj->ij', part, col_feat, precision=lax.Precision.HIGHEST)  6.41 us

profile of v1, /device:TPU:0, one launch (start us, length us, event | category | flops | bytes accessed | tf_op | source)
XLA Modules:
  0.0 175.2 jit_solution(14692213664940323825)
XLA Ops:
  0.0 32.5 %all-gather.2 = f32[8,96,32]{1,2,0:T(8,128)S(1)} all-gather(f32[1,96,32]{1,2,0:T(8,128)} %bitcast.84), channel_id=1, replica_groups=mesh['row'=8,'col'=4] {'row'}, dimensions={0}, use_global_device_ids=true | all-gather | bytes 110592 | tf_op jit(solution)/shard_map/all_gather | solution.py:23
  32.5 0.1 copy.13
  32.6 0.1 reshape.34
  32.8 0.7 copy-done
  33.4 5.2 %all-gather.1 = f32[4,96,32]{1,2,0:T(8,128)S(1)} all-gather(f32[1,96,32]{1,2,0:T(8,128)S(1)} %bitcast.85), channel_id=1, replica_groups=mesh['row'=8,'col'=4] {'col'}, dimensions={0}, use_global_device_ids=true | all-gather | bytes 61440 | tf_op jit(solution)/shard_map/all_gather | solution.py:70
  38.7 0.1 reshape.32
  38.9 19.3 %while.32 = (s32[]{:T(128)}, f32[3,128]{1,0:T(4,128)S(1)}, f32[3,768]{1,0:T(4,128)S(1)}, s32[3]{0:T(128)S(1)}, s32[3]{0:T(128)S(1)}, /*index=5*/f32[384]{0:T(512...) while((s32[]{:T(128)}, f32[3,128]{1,0:T(4,128)S(1)}, ...), condition=%wide.region_5.6_spmd, body=%wide.region_2.5_spmd.sunk | while | flops 38632584 | bytes 137449 | solution.py:39
  38.9 0.7 dynamic_slice.87
  41.6 0.7 dynamic_slice.88
  44.4 0.1 dynamic_slice.89
  44.5 0.7 fusion.51
  45.3 0.7 dynamic_slice.87
  48.1 0.7 dynamic_slice.88
  50.9 0.7 fusion.51
  51.8 0.7 dynamic_slice.87
  54.5 0.7 dynamic_slice.88
  57.3 0.7 fusion.51
  58.2 30.5 %all-gather.3 = f32[8,1,768]{2,1,0:T(1,128)S(1)} all-gather(f32[1,1,768]{2,1,0:T(1,128)S(1)} %reshape.35), channel_id=2, replica_groups=mesh['row'=8,'col'=4] {'row'}, dimensions={0}, use_global_device_ids=true | all-gather | bytes 27648 | tf_op jit(solution)/shard_map/all_gather | solution.py:42
  88.8 19.1 %while.33 = (s32[]{:T(128)}, f32[3,128]{1,0:T(4,128)S(1)}, s32[3]{0:T(128)S(1)}, s32[3]{0:T(128)S(1)}, f32[384]{0:T(512)S(1)}, /*index=5*/f32[768]{0:T(1024)S(1)...) while((s32[]{:T(128)}, f32[3,128]{1,0:T(4,128)S(1)}, ...), condition=%wide.region_11.12_spmd, body=%wide.region_9.11_spmd.sunk | while | flops 38633352 | bytes 132337 | solution.py:48
  88.8 0.7 dynamic_slice.91
  91.6 0.7 dynamic_slice.92
  94.4 0.7 fusion.54
  95.2 0.7 dynamic_slice.91
  97.9 0.7 dynamic_slice.92
  100.8 0.7 fusion.54
  101.5 0.7 dynamic_slice.91
  104.3 0.7 dynamic_slice.92
  107.1 0.7 fusion.54
  107.9 5.7 %all-reduce = (f32[1,384]{1,0:T(1,128)S(1)}, f32[1,384]{1,0:T(1,128)S(1)}) all-reduce(f32[1,384]{1,0:T(1,128)S(1)} %get-tuple-element.209, f32[1,384]{1,0:T(1,128)S(1)} %get-tuple-element.210), channel_id=1, replica_groups=mesh['row'=8,'col'=4] {'col'}, use_global_device_ids=true, to_apply=%region_12.13 | all-reduce | flops 768 | bytes 6144 | tf_op jit(solution)/shard_map/psum | solution.py:17
  113.7 0.6 copy-done.1
  114.3 30.6 %all-gather.4 = bf16[8,96,16]{1,2,0:T(8,128)(2,1)S(1)} all-gather(bf16[1,96,16]{1,2,0:T(8,128)(2,1)S(1)} %fusion.26), channel_id=1, replica_groups=mesh['row'=8,'col'=4] {'row'}, dimensions={0}, use_global_device_ids=true | all-gather | bytes 27648 | tf_op jit(solution)/shard_map/all_gather | solution.py:52
  144.9 0.1 reshape.38
  145.0 19.2 %while.34 = (s32[]{:T(128)}, f32[3,16,128]{2,1,0:T(8,128)S(1)}, s32[3]{0:T(128)S(1)}, s32[3]{0:T(128)S(1)}, f32[384]{0:T(512)S(1)}, /*index=5*/f32[768]{0:T(1024...) while((s32[]{:T(128)}, f32[3,16,128]{2,1,0:T(8,128)S(1)}, ...), condition=%wide.region_14.15_spmd, body=%wide.region_13.14_spmd.sunk | while | flops 41484296 | bytes 546533 | solution.py:59
  145.0 0.7 dynamic_slice.95
  147.8 0.7 dynamic_slice.96
  150.5 0.1 dynamic_slice.97
  150.6 0.6 fusion.59
  151.2 0.1 fusion.60
  151.4 0.7 dynamic_slice.95
  154.2 0.7 dynamic_slice.96
  157.0 0.6 fusion.59
  157.6 0.1 fusion.60
  157.8 0.7 dynamic_slice.95
  160.6 0.7 dynamic_slice.96
  163.4 0.6 fusion.59
  164.1 0.1 fusion.60
  164.2 10.3 %psum.23 = f32[16,384]{1,0:T(8,128)S(1)} all-reduce(f32[16,384]{1,0:T(8,128)S(1)} %copy_bitcast_fusion), channel_id=1, replica_groups=mesh['row'=8,'col'=4] {'col'}, use_global_device_ids=true, to_apply=%region_15.16 | all-reduce | flops 6144 | bytes 49152 | tf_op jit(solution)/shard_map/psum | solution.py:17
  174.5 0.7 dynamic-slice_multiply_fusion
  (45 shorter events, 1.3 us)
Async XLA Ops:
  32.7 0.7 copy-start
  113.6 0.7 copy-start.1
